TPU v7x, 32 devices: a whole 2x2x4 slice. The times are simulated.
32 devices in a mesh: dp: 8 (over y, x, core), expert: 4 (over z).
Axes of the slice: x: 2, y: 2, z: 4, core: 2. Of those that a mesh axis runs over, the one named last changes fastest.
Arguments:
- tokens: bfloat16 [512, 2048], P('expert', 'dp'), may hold values from -6 to 6
- routes: int32 [512, 2], P('expert'), may hold values from 0 to 3, all different within a row
- dt_raw: float32 [512, 32], P('expert', 'dp'), may hold values from -5 to 5
- b_proj: float32 [512, 16], P('expert'), may hold values from -1.8 to 1.8
- c_proj: float32 [512, 16], P('expert'), may hold values from -1.8 to 1.8
- decay_rate: float32 [32], P('dp'), may hold values from 0.002 to 0.2
- skip_gain: float32 [32], P('dp'), may hold values from 0.5 to 1.5
- router_weight: float32 [2048, 4], P('dp'), may hold values from -0.125 to 0.125
- gate_weight: bfloat16 [4, 2048, 7168], P('expert', None, 'dp'), may hold values from -0.125 to 0.125
- up_weight: bfloat16 [4, 2048, 7168], P('expert', None, 'dp'), may hold values from -0.125 to 0.125
- down_weight: bfloat16 [4, 7168, 2048], P('expert', 'dp'), may hold values from -0.0625 to 0.0625
- out_grad: bfloat16 [512, 2048], P('expert', 'dp'), may hold values from -6 to 6
Outputs:
- block_out: bfloat16 [512, 2048], P('expert', 'dp')
- token_grad: bfloat16 [512, 2048], P('expert', 'dp')
- gate_grad: bfloat16 [4, 2048, 7168], P('expert', None, 'dp')
- up_grad: bfloat16 [4, 2048, 7168], P('expert', None, 'dp')
- down_grad: bfloat16 [4, 7168, 2048], P('expert', 'dp')
- router_grad: float32 [2048, 4], P('dp')
- rate_grad: float32 [32], P('dp')
- skip_grad: float32 [32], P('dp')
Inputs may be any that keep to these rules, and one draw needn't show every extreme that they name: `routes`: each token names two different experts.
All inputs are finite; a program needn't handle non-finite values.
Results may differ from a plain program's by a relative error of at most 0.02.
Values may be sent and summed in bfloat16 or wider, within the bound.
A program may use at most 64 MiB of HBM per device.

v0:
```python
import jax
import jax.numpy as jnp
from jax import lax
from jax.sharding import PartitionSpec as P

D = 2048


EPSILON = 1e-06
HIGHEST = lax.Precision.HIGHEST


def carried_in(x, axis, combine, identity, reverse):
    peers, place = (lax.axis_size(axis), lax.axis_index(axis))
    everything = jax.tree.map(lambda part: lax.all_gather(part, axis), x)
    start = jax.tree.map(
        lambda part, zero: jnp.broadcast_to(jnp.asarray(zero, part.dtype), part.shape), x, identity
    )

    def lap(k, before):
        at = peers - 1 - k if reverse else k
        reached = at > place if reverse else at < place
        new = combine(before, jax.tree.map(lambda part: part[at], everything))
        return jax.tree.map(lambda a, b: jnp.where(reached, a, b), new, before)

    return lax.fori_loop(0, peers, lap, start)


def end_parts(normed, b_rows, dt_rows, decay_rate):
    steps_total = normed.shape[0]
    head_count = decay_rate.shape[0]
    step_size = jax.nn.softplus(dt_rows)
    running = jnp.cumsum(-step_size * decay_rate[None, :], axis=0)
    tail_weight = jnp.exp(running[-1][None, :] - running) * step_size
    head_rows = normed.reshape(steps_total, head_count, -1)
    local_state = jnp.einsum("sh,shp,sn->hpn", tail_weight, head_rows, b_rows, precision=HIGHEST)
    return (jnp.exp(running[-1]), local_state.reshape(head_count, -1))


def ssd_piece(normed, b_rows, c_rows, dt_rows, decay_rate, skip_gain, state_start):
    steps_total = normed.shape[0]
    head_count = decay_rate.shape[0]
    state_width = b_rows.shape[1]
    step_size = jax.nn.softplus(dt_rows)
    running = jnp.cumsum(-step_size * decay_rate[None, :], axis=0)
    positions = jnp.arange(steps_total, dtype=jnp.int32)
    causal = (positions[:, None] >= positions[None, :])[:, :, None]
    spread = jnp.where(causal, running[:, None, :] - running[None, :, :], 0.0)
    decay_table = jnp.where(causal, jnp.exp(spread), 0.0)
    pairing = jnp.dot(c_rows, b_rows.T, precision=HIGHEST)
    mixing = decay_table * pairing[:, :, None] * step_size[None, :, :]
    head_rows = normed.reshape(steps_total, head_count, -1)
    state_three = state_start.reshape(head_count, -1, state_width)
    mixed = jnp.einsum("tsh,shp->thp", mixing, head_rows, precision=HIGHEST)
    mixed = mixed + jnp.einsum(
        "tn,th,hpn->thp", c_rows, jnp.exp(running), state_three, precision=HIGHEST
    )
    mixed = mixed + skip_gain[None, :, None] * head_rows
    decay_total, local_state = end_parts(normed, b_rows, dt_rows, decay_rate)
    state_end = decay_total[:, None] * state_start + local_state
    return (mixed.reshape(steps_total, -1), state_end)


def dispatch_table(choice_ids, expert_count, capacity):
    flat_ids = choice_ids.reshape(-1)
    row_total = flat_ids.shape[0]
    expert_hot = (flat_ids[:, None] == jnp.arange(expert_count, dtype=jnp.int32)[None, :]).astype(
        jnp.float32
    )
    positions = jnp.arange(row_total, dtype=jnp.int32)
    lower = (positions[:, None] > positions[None, :]).astype(jnp.float32)
    earlier = jnp.dot(lower, expert_hot, precision=HIGHEST)
    slot_index = jnp.sum(earlier * expert_hot, axis=1)
    target = flat_ids.astype(jnp.float32) * capacity + slot_index
    target = jnp.where(slot_index < capacity, target, -1.0)
    slot_ids = jnp.arange(expert_count * capacity, dtype=jnp.int32).astype(jnp.float32)
    return (slot_ids[:, None] == target[None, :]).astype(jnp.float32)


def feature_sum(values):
    return lax.psum(values, "dp")


def norm_scale(values):
    total = feature_sum(jnp.sum(values * values, axis=-1, keepdims=True))
    return lax.rsqrt(total / D + EPSILON)


def norm_back(values, scale, grad):
    inner = feature_sum(jnp.sum(grad * values, axis=-1, keepdims=True))
    return scale * grad - values * (scale * scale * scale) * (inner / D)


def link_states(earlier, later):
    return (earlier[0] * later[0], later[0][:, None] * earlier[1] + later[1])


def carry_states(decay_total, state_part, backward):
    identity = (jnp.ones_like(decay_total), jnp.zeros_like(state_part))
    result = carried_in((decay_total, state_part), "expert", link_states, identity, backward)
    return result[1]


def to_units(send_rows):
    arrived = lax.all_to_all(send_rows, "expert", split_axis=0, concat_axis=0, tiled=True)
    flat_rows = arrived.reshape(-1, arrived.shape[2])
    return lax.all_gather(flat_rows, "dp", axis=1, tiled=True)


def from_units(terms, expert_count):
    summed = lax.psum_scatter(
        terms.astype(jnp.bfloat16), "dp", scatter_dimension=1, tiled=True
    ).astype(jnp.float32)
    shaped = summed.astype(jnp.bfloat16).reshape(expert_count, -1, summed.shape[1])
    returned = lax.all_to_all(shaped, "expert", split_axis=0, concat_axis=0, tiled=True)
    return returned.reshape(-1, summed.shape[1])


def body(
    tokens,
    routes,
    dt_raw,
    b_proj,
    c_proj,
    decay_rate,
    skip_gain,
    router_weight,
    gate_weight,
    up_weight,
    down_weight,
    out_grad,
):
    tok_count = tokens.shape[0]
    feature_count = tokens.shape[1]
    expert_count = lax.axis_size("expert")
    capacity = 5 * tok_count // (2 * expert_count)
    inputs = tokens.astype(jnp.float32)
    scale_one = norm_scale(inputs)
    normed = inputs * scale_one
    decay_total, local_state = end_parts(normed, b_proj, dt_raw, decay_rate)
    state_in = carry_states(decay_total, local_state, False)

    def mixer(normed_in, rate_in, skip_in, state_start):
        return ssd_piece(normed_in, b_proj, c_proj, dt_raw, rate_in, skip_in, state_start)

    (mixed, state_end), mixer_pull = jax.vjp(mixer, normed, decay_rate, skip_gain, state_in)
    resid = (inputs + mixed).astype(jnp.bfloat16)
    resid_f = resid.astype(jnp.float32)
    scale_two = norm_scale(resid_f)
    moe_in = (resid_f * scale_two).astype(jnp.bfloat16)
    moe_f = moe_in.astype(jnp.float32)
    logits = feature_sum(jnp.dot(moe_f, router_weight, precision=HIGHEST))
    expert_ids = jnp.arange(expert_count, dtype=jnp.int32)
    first_hot = (routes[:, 0:1] == expert_ids[None, :]).astype(jnp.float32)
    second_hot = (routes[:, 1:2] == expert_ids[None, :]).astype(jnp.float32)
    logit_gap = jnp.sum(logits * (first_hot - second_hot), axis=1)
    first_weight = jax.nn.sigmoid(logit_gap)
    second_weight = jax.nn.sigmoid(-logit_gap)
    table_b = dispatch_table(routes, expert_count, capacity).astype(jnp.bfloat16)
    doubled = jnp.repeat(moe_in, 2, axis=0)
    send_rows = jnp.dot(table_b, doubled, preferred_element_type=jnp.float32).astype(jnp.bfloat16)
    unit_rows = to_units(send_rows.reshape(expert_count, capacity, feature_count))
    gate_pre = jnp.dot(unit_rows, gate_weight[0], preferred_element_type=jnp.float32)
    up_pre = jnp.dot(unit_rows, up_weight[0], preferred_element_type=jnp.float32)
    hidden = (jax.nn.silu(gate_pre) * up_pre).astype(jnp.bfloat16)
    down_terms = jnp.dot(hidden, down_weight[0], preferred_element_type=jnp.float32)
    back_rows = from_units(down_terms, expert_count)
    per_slot = lax.dot_general(
        table_b, back_rows, (((0,), (0,)), ((), ())), preferred_element_type=jnp.float32
    )
    per_slot = per_slot.reshape(tok_count, 2, feature_count)
    moe_sum = first_weight[:, None] * per_slot[:, 0] + second_weight[:, None] * per_slot[:, 1]
    block_out = (resid_f + moe_sum).astype(jnp.bfloat16)
    upstream = out_grad.astype(jnp.float32)
    back_pair = feature_sum(jnp.sum(upstream[:, None, :] * per_slot, axis=2))
    first_back = back_pair[:, 0]
    second_back = back_pair[:, 1]
    slot_grad = jnp.stack(
        [first_weight[:, None] * upstream, second_weight[:, None] * upstream], axis=1
    )
    slot_grad = slot_grad.reshape(2 * tok_count, feature_count).astype(jnp.bfloat16)
    grad_send = jnp.dot(table_b, slot_grad, preferred_element_type=jnp.float32).astype(jnp.bfloat16)
    grad_rows = to_units(grad_send.reshape(expert_count, capacity, feature_count))
    unit_grad = lax.dot_general(
        grad_rows, down_weight[0], (((1,), (1,)), ((), ())), preferred_element_type=jnp.float32
    )
    sigma = jax.nn.sigmoid(gate_pre)
    gate_back = (unit_grad * up_pre * sigma * (1.0 + gate_pre * (1.0 - sigma))).astype(jnp.bfloat16)
    up_back = (unit_grad * jax.nn.silu(gate_pre)).astype(jnp.bfloat16)
    down_part = lax.dot_general(
        hidden, grad_rows, (((0,), (0,)), ((), ())), preferred_element_type=jnp.float32
    )
    gate_part = lax.dot_general(
        unit_rows, gate_back, (((0,), (0,)), ((), ())), preferred_element_type=jnp.float32
    )
    up_part = lax.dot_general(
        unit_rows, up_back, (((0,), (0,)), ((), ())), preferred_element_type=jnp.float32
    )
    gate_done = gate_part.astype(jnp.bfloat16)
    up_done = up_part.astype(jnp.bfloat16)
    down_done = down_part.astype(jnp.bfloat16)
    gate_side = lax.dot_general(
        gate_back, gate_weight[0], (((1,), (1,)), ((), ())), preferred_element_type=jnp.float32
    )
    up_side = lax.dot_general(
        up_back, up_weight[0], (((1,), (1,)), ((), ())), preferred_element_type=jnp.float32
    )
    returned = from_units(gate_side + up_side, expert_count)
    slot_back = lax.dot_general(
        table_b, returned, (((0,), (0,)), ((), ())), preferred_element_type=jnp.float32
    )
    slot_back = slot_back.reshape(tok_count, 2, feature_count)
    moe_grad = slot_back[:, 0] + slot_back[:, 1]
    gap_grad = first_weight * second_weight * (first_back - second_back)
    logit_grad = gap_grad[:, None] * (first_hot - second_hot)
    moe_in_grad = moe_grad + jnp.dot(logit_grad, router_weight.T, precision=HIGHEST)
    router_part = jnp.dot(moe_f.T, logit_grad, precision=HIGHEST)
    resid_grad = upstream + norm_back(resid_f, scale_two, moe_in_grad)
    zero_state = jnp.zeros_like(state_end)
    local_pull = mixer_pull((resid_grad, zero_state))
    later_grad = carry_states(decay_total, local_pull[3], True)
    tail_pull = mixer_pull((jnp.zeros_like(resid_grad), later_grad))
    normed_grad = local_pull[0] + tail_pull[0]
    rate_part = local_pull[1] + tail_pull[1]
    skip_part = local_pull[2] + tail_pull[2]
    token_grad = (resid_grad + norm_back(inputs, scale_one, normed_grad)).astype(jnp.bfloat16)
    router_total, rate_total, skip_total = lax.psum((router_part, rate_part, skip_part), "expert")
    return (
        block_out,
        token_grad,
        gate_done[None],
        up_done[None],
        down_done[None],
        router_total,
        rate_total,
        skip_total,
    )


def solution(mesh):
    return jax.shard_map(
        body,
        mesh=mesh,
        in_specs=(
            P("expert", "dp"),
            P("expert", None),
            P("expert", "dp"),
            P("expert", None),
            P("expert", None),
            P("dp"),
            P("dp"),
            P("dp", None),
            P("expert", None, "dp"),
            P("expert", None, "dp"),
            P("expert", "dp", None),
            P("expert", "dp"),
        ),
        out_specs=(
            P("expert", "dp"),
            P("expert", "dp"),
            P("expert", None, "dp"),
            P("expert", None, "dp"),
            P("expert", "dp", None),
            P("dp", None),
            P("dp"),
            P("dp"),
        ),
        check_vma=False,
    )
```

profile of v0, /device:TPU:0, one launch (start us, length us, event | category | flops | bytes accessed | tf_op | source)
XLA Modules:
  0.0 330.2 jit_solution(9613662080499625949)
XLA Ops:
  7.3 0.7 compare_select_fusion
  8.4 0.9 fusion.60
  9.4 15.2 %psum.63 = f32[128,1]{0,1:T(1,128)S(1)} all-reduce(f32[128,1]{0,1:T(1,128)S(1)} %bitcast.271), channel_id=1, replica_groups=mesh['dp'=8,'expert'=4] {'dp'}, use_global_device_ids=true, to_apply=%region_1.0 | all-reduce | flops 128 | bytes 1024 | tf_op jit(solution)/shard_map/psum | solution.py:81
  24.8 11.2 %all-gather = f32[4,1,4]{2,1,0:T(1,128)S(1)} all-gather(f32[1,1,4]{2,1,0:T(1,128)S(1)} %bitcast.267), channel_id=1, replica_groups=mesh['dp'=8,'expert'=4] {'expert'}, dimensions={0}, use_global_device_ids=true | all-gather | bytes 80 | tf_op jit(solution)/shard_map/all_gather | solution.py:15
  35.9 0.7 fusion.132
  36.7 0.8 copy.172
  37.9 0.9 convert_multiply_fusion.6
  38.9 1.0 fusion.156
  40.3 13.1 %all_gather.20 = f32[4,4,1024]{2,1,0:T(4,128)S(1)} all-gather(f32[1,4,1024]{2,1,0:T(4,128)S(1)} %all_gather_reshape.3), channel_id=1, replica_groups=mesh['dp'=8,'expert'=4] {'expert'}, dimensions={0}, use_global_device_ids=true | all-gather | bytes 81920 | tf_op jit(solution)/shard_map/all_gather | solution.py:15
  54.2 0.7 fusion.40
  55.1 11.8 %psum.64 = f32[128,1]{0,1:T(1,128)S(1)} all-reduce(f32[128,1]{0,1:T(1,128)S(1)} %bitcast.269), channel_id=1, replica_groups=mesh['dp'=8,'expert'=4] {'dp'}, use_global_device_ids=true, to_apply=%region_6.7 | all-reduce | flops 128 | bytes 1024 | tf_op jit(solution)/shard_map/psum | solution.py:81
  67.4 10.0 %all_to_all.20 = bf16[4,80,256]{2,1,0:T(8,128)(2,1)} all-to-all(bf16[4,80,256]{2,1,0:T(8,128)(2,1)S(1)} %bitcast.259), channel_id=1, replica_groups=mesh['dp'=8,'expert'=4] {'expert'}, dimensions={0} | all-to-all | bytes 327680 | tf_op jit(solution)/shard_map/all_to_all | solution.py:105
  77.6 22.0 %all-gather.4.cloned.1.call-done = bf16[320,2048]{1,0:T(8,128)(2,1)} async-done(((bf16[320,256]{1,0:T(8,128)(2,1)}), bf16[320,2048]{1,0:T(8,128)(2,1)}) %all-gather.4.cloned.1.call-update) | async-done | bytes 1310736 | tf_op jit(solution)/shard_map/all_gather | solution.py:107
  99.6 4.1 %fusion.12 = f32[320,896]{1,0:T(8,128)S(1)} fusion(bf16[320,2048]{1,0:T(8,128)(2,1)} %all-gather.4.cloned.1.call-done, bf16[1,2048,896]{2,1,0:T(8,128)(2,1)} %param.24), kind=kOutput, calls=%fused_computation.16 | convolution fusion | flops 1174405120 | bytes 6127616 | tf_op jit(solution)/shard_map/dot_general | solution.py:163
  103.7 2.6 multiply_convert_fusion.2
  106.3 0.8 copy-done.14
  107.2 2.6 fusion.20
  110.0 0.5 copy-done.6
  110.6 36.6 %reduce-scatter.3.cloned.1.call-done = bf16[320,256]{1,0:T(8,128)(2,1)} async-done(((bf16[320,2048]{1,0:T(8,128)(2,1)}), bf16[320,256]{1,0:T(8,128)(2,1)}) %reduce-scatter.3.cloned.1.call-update) | async-done | bytes 163856 | tf_op jit(solution)/shard_map/reduce_scatter | solution.py:111
  147.2 4.6 %all-to-all-start.1 = ((bf16[4,80,256]{2,1,0:T(8,128)(2,1)}), bf16[4,80,256]{2,1,0:T(8,128)(2,1)S(1)}, u32[]{:S(2)}, u32[]{:S(2)}) async-start(bf16[4,80,256]{2,1,0:T(8,128)(2,1)} %bitcast.257), calls=%async_computation.2 | async-start | bytes 327680 | tf_op jit(solution)/shard_map/all_to_all | solution.py:115
  152.0 6.2 %all-to-all-done.1 = bf16[4,80,256]{2,1,0:T(8,128)(2,1)S(1)} async-done(((bf16[4,80,256]{2,1,0:T(8,128)(2,1)}), bf16[4,80,256]{2,1,0:T(8,128)(2,1)S(1)}, u32[]{:S(2)}, u32[]{:S(2)}) %all-to-all-start.1) | async-done | bytes 163872 | tf_op jit(solution)/shard_map/all_to_all | solution.py:115
  158.6 11.8 %all-reduce.4 = (f32[128,4]{0,1:T(4,128)S(1)}, f32[128,2]{0,1:T(2,128)S(1)}) all-reduce(f32[128,4]{0,1:T(4,128)S(1)} %fusion.157, f32[128,2]{0,1:T(2,128)S(1)} %get-tuple-element.343), channel_id=1, replica_groups=mesh['dp'=8,'expert'=4] {'dp'}, use_global_device_ids=true, to_apply=%region_7.8 | all-reduce | flops 768 | bytes 6144 | tf_op jit(solution)/shard_map/psum | solution.py:81
  171.1 10.0 %all_to_all.21 = bf16[4,80,256]{2,1,0:T(8,128)(2,1)} all-to-all(bf16[4,80,256]{2,1,0:T(8,128)(2,1)S(1)} %bitcast.258), channel_id=1, replica_groups=mesh['dp'=8,'expert'=4] {'expert'}, dimensions={0} | all-to-all | bytes 327680 | tf_op jit(solution)/shard_map/all_to_all | solution.py:105
  181.4 22.7 %all-gather.6.cloned.1.call-done = bf16[320,2048]{1,0:T(8,128)(2,1)} async-done(((bf16[320,256]{1,0:T(8,128)(2,1)}), bf16[320,2048]{1,0:T(8,128)(2,1)}) %all-gather.6.cloned.1.call-update) | async-done | bytes 1310736 | tf_op jit(solution)/shard_map/all_gather | solution.py:107
  204.1 5.0 %multiply_convert_fusion.1 = (bf16[320,896]{1,0:T(8,128)(2,1)S(1)}, bf16[320,896]{1,0:T(8,128)(2,1)S(1)}) fusion(f32[320,896]{1,0:T(8,128)} %copy-done.13, f32[320,896]{1,0:T(8,128)} %get-tuple-element.342, bf16[320,2048]{1,0:T(8,128)(2,1)} %all-gather.6.cloned.1.call-done, bf16[1,896,2048]{2,1,0:T(8,128)(2,1)} %param.26), kind=kOutput, calls=%fused_computation.39 | convolution fusion | flops 1178132480 | bytes 8421376 | tf_op jit(solution)/shard_map/dot_general | solution.py:184
  209.1 1.6 fusion.6
  210.7 0.6 copy-done.10
  211.4 2.6 fusion.17
  214.0 0.5 fusion.152
  215.7 5.5 %convert_bitcast_fusion = bf16[1,896,2048]{2,1,0:T(8,128)(2,1)} fusion(bf16[320,896]{1,0:T(8,128)(2,1)} %copy-done.14, bf16[320,2048]{1,0:T(8,128)(2,1)} %all-gather.6.cloned.1.call-done), kind=kOutput, calls=%fused_computation.18 | convolution fusion | flops 1176240128 | bytes 5554176 | tf_op jit(solution)/shard_map/dot_general | solution.py:190
  221.3 4.1 %convert_bitcast_fusion.2 = bf16[1,2048,896]{2,1,0:T(8,128)(2,1)} fusion(bf16[320,2048]{1,0:T(8,128)(2,1)S(1)} %copy-done.11, bf16[320,896]{1,0:T(8,128)(2,1)S(1)} %copy-done.16), kind=kOutput, calls=%fused_computation.20 | convolution fusion | flops 1176240128 | bytes 5554176 | tf_op jit(solution)/shard_map/dot_general | solution.py:193
  225.4 26.0 %reduce-scatter.5.cloned.1.call-done = bf16[320,256]{1,0:T(8,128)(2,1)} async-done(((bf16[320,2048]{1,0:T(8,128)(2,1)}), bf16[320,256]{1,0:T(8,128)(2,1)}) %reduce-scatter.5.cloned.1.call-update) | async-done | bytes 163856 | tf_op jit(solution)/shard_map/reduce_scatter | solution.py:111
  251.4 4.6 %all-to-all-start.3 = ((bf16[4,80,256]{2,1,0:T(8,128)(2,1)}), bf16[4,80,256]{2,1,0:T(8,128)(2,1)S(1)}, u32[]{:S(2)}, u32[]{:S(2)}) async-start(bf16[4,80,256]{2,1,0:T(8,128)(2,1)} %bitcast.256), calls=%async_computation.5 | async-start | bytes 327680 | tf_op jit(solution)/shard_map/all_to_all | solution.py:115
  256.0 4.1 %convert_bitcast_fusion.1 = bf16[1,2048,896]{2,1,0:T(8,128)(2,1)} fusion(bf16[320,2048]{1,0:T(8,128)(2,1)S(1)} %copy-done.11, bf16[320,896]{1,0:T(8,128)(2,1)S(1)} %get-tuple-element.322), kind=kOutput, calls=%fused_computation.19 | convolution fusion | flops 1176240128 | bytes 5554176 | tf_op jit(solution)/shard_map/dot_general | solution.py:196
  260.1 2.3 all-to-all-done.3
  263.2 12.0 %psum.67 = f32[128,1]{0,1:T(1,128)S(1)} all-reduce(f32[128,1]{0,1:T(1,128)S(1)} %bitcast.268), channel_id=1, replica_groups=mesh['dp'=8,'expert'=4] {'dp'}, use_global_device_ids=true, to_apply=%region_15.16 | all-reduce | flops 128 | bytes 1024 | tf_op jit(solution)/shard_map/psum | solution.py:81
  275.2 0.8 fusion.72
  276.9 13.1 %all_gather.23 = f32[4,4,1024]{2,1,0:T(4,128)S(1)} all-gather(f32[1,4,1024]{2,1,0:T(4,128)S(1)} %broadcast_add_fusion), channel_id=1, replica_groups=mesh['dp'=8,'expert'=4] {'expert'}, dimensions={0}, use_global_device_ids=true | all-gather | bytes 81920 | tf_op jit(solution)/shard_map/all_gather | solution.py:15
  291.3 0.7 fusion.151
  292.6 1.1 reduce_window_sum.45
  293.9 1.1 reduce_window_sum.47
  295.3 0.5 fusion.38
  295.8 0.5 fusion.36
  296.9 11.8 %psum.68 = f32[128,1]{0,1:T(1,128)S(1)} all-reduce(f32[128,1]{0,1:T(1,128)S(1)} %bitcast.270), channel_id=1, replica_groups=mesh['dp'=8,'expert'=4] {'dp'}, use_global_device_ids=true, to_apply=%region_19.20 | all-reduce | flops 128 | bytes 1024 | tf_op jit(solution)/shard_map/psum | solution.py:81
  309.4 1.1 reduce_window_sum.46
  310.7 1.1 reduce_window_sum.44
  311.9 0.8 fusion.65
  312.8 10.8 %all-reduce.5 = (f32[256,4]{0,1:T(4,128)}, f32[4]{0:T(128)}, f32[4]{0:T(128)}) all-reduce(f32[256,4]{0,1:T(4,128)S(1)} %fusion.126, f32[4]{0:T(128)S(1)} %add_add_fusion, f32[4]{0:T(128)S(1)} %add.227), channel_id=1, replica_groups=mesh['dp'=8,'expert'=4] {'expert'}, use_global_device_ids=true, to_apply=%region_20.21 | all-reduce | flops 1032 | bytes 8256 | tf_op jit(solution)/shard_map/psum | solution.py:227
  (151 shorter events, 12.4 us)
Async XLA Ops:
  7.2 144.7 %copy-start = (f32[256,4]{0,1:T(4,128)S(1)}, f32[256,4]{0,1:T(4,128)}, u32[]{:S(2)}) copy-start(f32[256,4]{0,1:T(4,128)} %param.23) | copy-start | bytes 12292
  7.2 32.8 %copy-start.3 = (f32[128,16]{0,1:T(8,128)S(1)}, f32[128,16]{0,1:T(8,128)}, u32[]{:S(2)}) copy-start(f32[128,16]{0,1:T(8,128)} %param.19) | copy-start | bytes 24580
  7.2 46.7 %copy-start.4 = (f32[128,16]{0,1:T(8,128)S(1)}, f32[128,16]{0,1:T(8,128)}, u32[]{:S(2)}) copy-start(f32[128,16]{0,1:T(8,128)} %param.20) | copy-start | bytes 24580
  7.2 92.4 %all-gather.4.cloned.1.call-start = ((), (), s32[]{:S(2)}) async-start(), calls=%async_computation.6 | async-start | bytes 1474560 | tf_op jit(solution)/shard_map/all_gather | solution.py:107
  8.2 46.0 %copy-start.12 = (f32[4]{0:T(128)S(1)}, f32[4]{0:T(128)}, u32[]{:S(2)}) copy-start(f32[4]{0:T(128)} %param.22) | copy-start | bytes 52
  38.8 16.2 %copy-start.1 = (bf16[128,256]{1,0:T(8,128)(2,1)S(1)}, bf16[128,256]{1,0:T(8,128)(2,1)}, u32[]{:S(2)}) copy-start(bf16[128,256]{1,0:T(8,128)(2,1)} %param.16) | copy-start | bytes 196612
  77.5 69.7 %reduce-scatter.3.cloned.1.call-start = ((), (), s32[]{:S(2)}) async-start(), calls=%async_computation.7 | async-start | bytes 1474560 | tf_op jit(solution)/shard_map/reduce_scatter | solution.py:111
  99.6 4.1 %copy-start.8 = (bf16[1,2048,896]{2,1,0:T(8,128)(2,1)S(1)}, bf16[1,2048,896]{2,1,0:T(8,128)(2,1)}, u32[]{:S(2)}) copy-start(bf16[1,2048,896]{2,1,0:T(8,128)(2,1)} %param.25) | copy-start | bytes 11010052
  99.6 4.1 %copy-start.11 = (bf16[320,2048]{1,0:T(8,128)(2,1)S(1)}, bf16[320,2048]{1,0:T(8,128)(2,1)}, u32[]{:S(2)}) copy-start(bf16[320,2048]{1,0:T(8,128)(2,1)} %all-gather.4.cloned.1.call-done) | copy-start | bytes 3932164
  103.7 2.6 copy-start.13
  103.7 3.5 %copy-start.7 = (bf16[1,896,2048]{2,1,0:T(8,128)(2,1)S(1)}, bf16[1,896,2048]{2,1,0:T(8,128)(2,1)}, u32[]{:S(2)}) copy-start(bf16[1,896,2048]{2,1,0:T(8,128)(2,1)} %param.26) | copy-start | bytes 11010052
  106.3 0.8 copy-start.14
  109.8 0.7 copy-start.6
  109.8 42.0 %copy-start.2 = (bf16[128,256]{1,0:T(8,128)(2,1)S(1)}, bf16[128,256]{1,0:T(8,128)(2,1)}, u32[]{:S(2)}) copy-start(bf16[128,256]{1,0:T(8,128)(2,1)} %param.27) | copy-start | bytes 196612
  147.2 11.0 %all-to-all-start.1 = ((bf16[4,80,256]{2,1,0:T(8,128)(2,1)}), bf16[4,80,256]{2,1,0:T(8,128)(2,1)S(1)}, u32[]{:S(2)}, u32[]{:S(2)}) async-start(bf16[4,80,256]{2,1,0:T(8,128)(2,1)} %bitcast.257), calls=%async_computation.2 | async-start | bytes 327680 | tf_op jit(solution)/shard_map/all_to_all | solution.py:115
  151.8 52.3 %all-gather.6.cloned.1.call-start = ((), (), s32[]{:S(2)}) async-start(), calls=%async_computation.8 | async-start | bytes 1474560 | tf_op jit(solution)/shard_map/all_gather | solution.py:107
  181.1 70.2 %reduce-scatter.5.cloned.1.call-start = ((), (), s32[]{:S(2)}) async-start(), calls=%async_computation.9 | async-start | bytes 1474560 | tf_op jit(solution)/shard_map/reduce_scatter | solution.py:111
  204.1 5.0 %copy-start.9 = (bf16[1,2048,896]{2,1,0:T(8,128)(2,1)S(1)}, bf16[1,2048,896]{2,1,0:T(8,128)(2,1)}, u32[]{:S(2)}) copy-start(bf16[1,2048,896]{2,1,0:T(8,128)(2,1)} %param.25) | copy-start | bytes 11010052
  209.1 1.6 copy-start.15
  209.1 2.2 copy-start.10
  215.7 5.5 %copy-start.16 = (bf16[320,896]{1,0:T(8,128)(2,1)S(1)}, bf16[320,896]{1,0:T(8,128)(2,1)}, u32[]{:S(2)}) copy-start(bf16[320,896]{1,0:T(8,128)(2,1)} %copy-done.15) | copy-start | bytes 1720324
  251.4 11.0 %all-to-all-start.3 = ((bf16[4,80,256]{2,1,0:T(8,128)(2,1)}), bf16[4,80,256]{2,1,0:T(8,128)(2,1)S(1)}, u32[]{:S(2)}, u32[]{:S(2)}) async-start(bf16[4,80,256]{2,1,0:T(8,128)(2,1)} %bitcast.256), calls=%async_computation.5 | async-start | bytes 327680 | tf_op jit(solution)/shard_map/all_to_all | solution.py:115
  292.2 4.1 %copy-start.5 = (f32[128,4]{0,1:T(4,128)S(1)}, f32[128,4]{0,1:T(4,128)}, u32[]{:S(2)}) copy-start(f32[128,4]{0,1:T(4,128)} %param.18) | copy-start | bytes 6148
Sparse Core Ops, SparseCore 0:
  77.6 21.9 all-gather.3
  109.9 37.1 reduce-scatter.2
  181.2 22.7 all-gather.5
  214.1 37.1 reduce-scatter.4
where the time goes:
time: 331 us; the launch traced here: 330 us
  blocking collectives  131 us (40%)
  waiting for transfers between devices  116 us (35%)
  matrix products  40.8 us (12%)
  between operations  14.3 us (4%)
  other arithmetic  11.9 us (4%)
  starting transfers between devices  9.5 us (3%)
  local copies, waits for them, and re-layouts  6.81 us (2%)
    psum x5, blocking collectives, feature_sum(): return lax.psum(values, 'dp')  62.6 us
    reduce_scatter x2, waiting for transfers between devices, from_units(): lax.psum_scatter(terms.astype(jnp.bfloat16), 'dp', scatter_dimension=1, t...  62.5 us
    all_gather x2, waiting for transfers between devices, to_units(): return lax.all_gather(flat_rows, 'dp', axis=1, tiled=True)  44.8 us
    all_gather x3, blocking collectives, carried_in(): everything = jax.tree.map(lambda part: lax.all_gather(part, axis), x)  37.4 us
    all_to_all x2, blocking collectives, to_units(): lax.all_to_all(send_rows, 'expert', split_axis=0, concat_axis=0, tiled=True)  20.1 us
    psum x1, blocking collectives, body(): lax.psum((router_part, rate_part, skip_part), 'expert')  10.8 us
    all_to_all x2, starting transfers between devices, from_units(): lax.all_to_all(shaped, 'expert', split_axis=0, concat_axis=0, tiled=True)  9.2 us
    all_to_all x2, waiting for transfers between devices, from_units(): lax.all_to_all(shaped, 'expert', split_axis=0, concat_axis=0, tiled=True)  8.5 us
  transfers between devices with their start and end apart: 6, of which 6 were waited for; matrix products, arithmetic and copies ran while one was open for 5% of the time, Pallas kernels for 0%

commit v1 on v0

v1 whole, which is shorter than its diff:
```python
import functools
import jax
import jax.numpy as jnp
from jax import lax
from jax.experimental import pallas as pl
from jax.experimental.pallas import tpu as pltpu
from jax.sharding import PartitionSpec as P


EPSILON = 1e-06
HIGHEST = lax.Precision.HIGHEST
MESH = pl.DeviceIdType.MESH


def loop(count, step):
    def run(i, carry):
        step(i)
        return carry

    lax.fori_loop(0, count, run, 0)


def greet(axes):
    barrier = pltpu.get_barrier_semaphore()
    total = 0
    for axis in axes:
        peers, place = (lax.axis_size(axis), lax.axis_index(axis))
        total += peers - 1

        def signal(k):
            pl.semaphore_signal(
                barrier, 1, device_id={axis: lax.rem(place + k + 1, peers)}, device_id_type=MESH
            )

        loop(peers - 1, signal)
    pl.semaphore_wait(barrier, total)


def swap_kernel(plan, *refs):
    amount = len(plan)
    ins, outs = (refs[:amount], refs[amount : 2 * amount])
    gathered = refs[2 * amount : 3 * amount]
    sends, recvs = (refs[3 * amount : 4 * amount], refs[4 * amount : 5 * amount])
    greet(sorted({axis for axis, _ in plan}))

    def copy_of(item, k):
        axis = plan[item][0]
        peers, place = (lax.axis_size(axis), lax.axis_index(axis))
        return pltpu.make_async_remote_copy(
            src_ref=ins[item],
            dst_ref=gathered[item].at[place],
            send_sem=sends[item].at[k],
            recv_sem=recvs[item].at[k],
            device_id={axis: lax.rem(place + k + 1, peers)},
            device_id_type=MESH,
        )

    for item, (axis, _) in enumerate(plan):
        loop(lax.axis_size(axis) - 1, lambda k: copy_of(item, k).start())
        gathered[item][lax.axis_index(axis)] = ins[item][...]
    for item, (axis, reduce) in enumerate(plan):
        peers, place = (lax.axis_size(axis), lax.axis_index(axis))

        def arrive(k):
            pltpu.make_async_remote_copy(
                src_ref=ins[item],
                dst_ref=gathered[item].at[lax.rem(place + peers - k - 1, peers)],
                send_sem=sends[item].at[k],
                recv_sem=recvs[item].at[k],
                device_id={axis: lax.rem(place + k + 1, peers)},
                device_id_type=MESH,
            ).wait()

        loop(peers - 1, arrive)
        if reduce:
            outs[item][...] = jnp.sum(gathered[item][...], axis=0)
        else:
            outs[item][...] = gathered[item][...]


def swap(name, number, *items):
    plan = tuple((axis, reduce) for _, axis, reduce in items)
    arrays = [array for array, _, _ in items]
    full = [(lax.axis_size(axis),) + array.shape for array, axis, _ in items]
    kept = [array.shape if reduce else shape for (array, _, reduce), shape in zip(items, full)]
    sems = [pltpu.SemaphoreType.DMA((shape[0] - 1,)) for shape in full]
    return pl.pallas_call(
        functools.partial(swap_kernel, plan),
        out_shape=[jax.ShapeDtypeStruct(shape, jnp.float32) for shape in kept],
        in_specs=[pl.BlockSpec(memory_space=pltpu.VMEM)] * len(items),
        out_specs=[pl.BlockSpec(memory_space=pltpu.VMEM)] * len(items),
        scratch_shapes=[pltpu.VMEM(shape, jnp.float32) for shape in full] + sems + sems,
        compiler_params=pltpu.CompilerParams(collective_id=number, has_side_effects=True),
        name=name,
    )(*arrays)


def end_parts(normed, b_rows, dt_rows, decay_rate):
    steps_total = normed.shape[0]
    head_count = decay_rate.shape[0]
    step_size = jax.nn.softplus(dt_rows)
    running = jnp.cumsum(-step_size * decay_rate[None, :], axis=0)
    tail_weight = jnp.exp(running[-1][None, :] - running) * step_size
    head_rows = normed.reshape(steps_total, head_count, -1)
    local_state = jnp.einsum("sh,shp,sn->hpn", tail_weight, head_rows, b_rows, precision=HIGHEST)
    return (jnp.exp(running[-1]), local_state.reshape(head_count, -1))


def ssd_piece(normed, b_rows, c_rows, dt_rows, decay_rate, skip_gain, state_start):
    steps_total = normed.shape[0]
    head_count = decay_rate.shape[0]
    state_width = b_rows.shape[1]
    step_size = jax.nn.softplus(dt_rows)
    running = jnp.cumsum(-step_size * decay_rate[None, :], axis=0)
    positions = jnp.arange(steps_total, dtype=jnp.int32)
    causal = (positions[:, None] >= positions[None, :])[:, :, None]
    spread = jnp.where(causal, running[:, None, :] - running[None, :, :], 0.0)
    decay_table = jnp.where(causal, jnp.exp(spread), 0.0)
    pairing = jnp.dot(c_rows, b_rows.T, precision=HIGHEST)
    mixing = decay_table * pairing[:, :, None] * step_size[None, :, :]
    head_rows = normed.reshape(steps_total, head_count, -1)
    state_three = state_start.reshape(head_count, -1, state_width)
    mixed = jnp.einsum("tsh,shp->thp", mixing, head_rows, precision=HIGHEST)
    mixed = mixed + jnp.einsum(
        "tn,th,hpn->thp", c_rows, jnp.exp(running), state_three, precision=HIGHEST
    )
    mixed = mixed + skip_gain[None, :, None] * head_rows
    decay_total, local_state = end_parts(normed, b_rows, dt_rows, decay_rate)
    state_end = decay_total[:, None] * state_start + local_state
    return (mixed.reshape(steps_total, -1), state_end)


def carry_in(decays, states, reverse):
    peers, place = (lax.axis_size("expert"), lax.axis_index("expert"))
    held = jnp.zeros_like(states[0])
    for k in range(peers):
        at = peers - 1 - k if reverse else k
        reached = at > place if reverse else at < place
        held = jnp.where(reached, decays[at][:, None] * held + states[at], held)
    return held


def slices(total, width):
    return [(at, min(width, total - at)) for at in range(0, total, width)]


def expert_kernel(
    cap,
    send_rows,
    send_grads,
    gate_hbm,
    up_hbm,
    down_hbm,
    back_f,
    back_b,
    rows,
    grads,
    hidden,
    gate_back,
    up_back,
    gate_w,
    up_w,
    down_w,
    gate_s,
    up_s,
    away,
    mine,
    pair,
    chips,
    summed,
    z_send,
    z_recv,
    c_send,
    c_recv,
    p_send,
    p_recv,
    pair_send,
    pair_recv,
    chip_send,
    chip_recv,
    back_send,
    back_recv,
    local_sem,
    weight_sem,
):
    peers, place = (lax.axis_size("dp"), lax.axis_index("dp"))
    blocks, block = (lax.axis_size("expert"), lax.axis_index("expert"))
    chip_count = peers // 2
    chip, core = (place // 2, lax.rem(place, 2))
    partner = place + 1 - 2 * core
    width = send_rows.shape[1]
    units = gate_w.shape[1]
    sources = (send_rows, send_grads)
    wholes = (rows, grads)
    backs = (back_f, back_b)

    def strip(j):
        return pl.ds(pl.multiple_of(j * cap, 16), cap)

    def columns(d):
        return pl.ds(pl.multiple_of(d * width, 128), width)

    def ahead(k):
        return lax.rem(block + k, blocks)

    def chip_at(q):
        return lax.rem(chip + q, chip_count)

    weights = [
        pltpu.make_async_copy(hbm.at[0], held, weight_sem.at[n])
        for n, (hbm, held) in enumerate(
            ((gate_hbm, gate_w), (up_hbm, up_w), (down_hbm, down_w))
        )
    ]
    for item in weights:
        item.start()
    greet(("dp", "expert"))

    def own_copy(t):
        return pltpu.make_async_copy(
            sources[t].at[strip(block), :], wholes[t].at[strip(block), columns(place)], local_sem.at[t]
        )

    def z_copy(t, k, land):
        return pltpu.make_async_remote_copy(
            src_ref=sources[t].at[strip(ahead(k)), :],
            dst_ref=wholes[t].at[strip(land), columns(place)],
            send_sem=z_send.at[t, k],
            recv_sem=z_recv.at[t, k],
            device_id={"expert": ahead(k)},
            device_id_type=MESH,
        )

    def spread_copy(t, k, j, q, owner):
        cut = wholes[t].at[strip(j), columns(owner)]
        return pltpu.make_async_remote_copy(
            src_ref=cut,
            dst_ref=cut,
            send_sem=c_send.at[t, k * chip_count + q],
            recv_sem=c_recv.at[t, k * chip_count + q],
            device_id={"dp": 2 * chip_at(q) + core},
            device_id_type=MESH,
        )

    def partner_copy(t, k, j, q, owner):
        cut = wholes[t].at[strip(j), columns(owner)]
        return pltpu.make_async_remote_copy(
            src_ref=cut,
            dst_ref=cut,
            send_sem=p_send.at[t, k * chip_count + q],
            recv_sem=p_recv.at[t, k * chip_count + q],
            device_id={"dp": partner},
            device_id_type=MESH,
        )

    for t in range(2):
        own_copy(t).start()
        loop(blocks - 1, lambda k: z_copy(t, k + 1, block).start())

    def forward(t, k, j):
        loop(chip_count - 1, lambda q: spread_copy(t, k, j, q + 1, place).start())
        partner_copy(t, k, j, 0, place).start()

    for t in range(2):
        own_copy(t).wait()
        forward(t, 0, block)

        def pass_on(n):
            k = n + 1
            origin = lax.rem(block + blocks - k, blocks)
            z_copy(t, k, origin).wait_recv()
            forward(t, k, origin)

        loop(blocks - 1, pass_on)

    def origin_of(k):
        return lax.rem(block + blocks - k, blocks)

    def relay(t):
        def one(n):
            k, q = (n // (chip_count - 1), lax.rem(n, chip_count - 1) + 1)
            owner = 2 * lax.rem(chip + chip_count - q, chip_count) + core
            spread_copy(t, k, origin_of(k), q, owner).wait_recv()
            partner_copy(t, k, origin_of(k), q, owner).start()

        loop(blocks * (chip_count - 1), one)

        def last(n):
            k, q = (n // chip_count, lax.rem(n, chip_count))
            owner = 2 * lax.rem(chip + chip_count - q, chip_count) + 1 - core
            partner_copy(t, k, origin_of(k), q, owner).wait_recv()

        loop(blocks * chip_count, last)

    def pair_copy(t, c):
        return pltpu.make_async_remote_copy(
            src_ref=away.at[t, c],
            dst_ref=pair.at[t, c],
            send_sem=pair_send.at[t, c],
            recv_sem=pair_recv.at[t, c],
            device_id={"dp": partner},
            device_id_type=MESH,
        )

    def chip_copy(t, q):
        return pltpu.make_async_remote_copy(
            src_ref=mine.at[t, chip_at(q)],
            dst_ref=chips.at[t, q],
            send_sem=chip_send.at[t, q],
            recv_sem=chip_recv.at[t, q],
            device_id={"dp": 2 * chip_at(q) + core},
            device_id_type=MESH,
        )

    def back_copy(t, k, land):
        return pltpu.make_async_remote_copy(
            src_ref=summed.at[t, strip(ahead(k)), :],
            dst_ref=backs[t].at[strip(land), :],
            send_sem=back_send.at[t, k],
            recv_sem=back_recv.at[t, k],
            device_id={"expert": ahead(k)},
            device_id_type=MESH,
        )

    def tiles(t, term):
        def for_partner(q):
            c = chip_at(lax.rem(q + 1, chip_count))
            away[t, c] = term(2 * c + 1 - core).astype(jnp.bfloat16)
            pair_copy(t, c).start()

        loop(chip_count, for_partner)

        def for_mine(q):
            c = chip_at(lax.rem(q + 1, chip_count))
            value = term(2 * c + core)
            pair_copy(t, c).wait_recv()
            mine[t, c] = (value + pair[t, c].astype(jnp.float32)).astype(jnp.bfloat16)

            @pl.when(q < chip_count - 1)
            def _():
                chip_copy(t, q + 1).start()

        loop(chip_count, for_mine)

    def finish(t):
        total = mine[t, chip].astype(jnp.float32)
        for q in range(1, chip_count):
            chip_copy(t, q).wait_recv()
            total = total + chips[t, q].astype(jnp.float32)
        summed[t] = total.astype(jnp.bfloat16)
        loop(blocks - 1, lambda k: back_copy(t, k + 1, block).start())
        backs[t][strip(block), :] = summed[t, strip(block), :]

    relay(0)
    weights[0].wait()
    weights[1].wait()
    for at, span in slices(units, 256):
        cut = slice(at, at + span)
        gate = jnp.dot(rows[...], gate_w[:, cut], preferred_element_type=jnp.float32)
        up = jnp.dot(rows[...], up_w[:, cut], preferred_element_type=jnp.float32)
        gate_s[:, cut] = gate
        up_s[:, cut] = up
        hidden[:, cut] = (gate * jax.nn.sigmoid(gate) * up).astype(jnp.bfloat16)
    weights[2].wait()
    tiles(
        0,
        lambda d: jnp.dot(hidden[...], down_w[:, columns(d)], preferred_element_type=jnp.float32),
    )
    relay(1)
    nt = (((1,), (1,)), ((), ()))
    for at, span in slices(units, 256):
        cut = slice(at, at + span)
        unit_grad = lax.dot_general(
            grads[...], down_w[cut, :], nt, preferred_element_type=jnp.float32
        )
        gate = gate_s[:, cut]
        sigma = jax.nn.sigmoid(gate)
        gate_back[:, cut] = (
            unit_grad * up_s[:, cut] * sigma * (1.0 + gate * (1.0 - sigma))
        ).astype(jnp.bfloat16)
        up_back[:, cut] = (unit_grad * gate * sigma).astype(jnp.bfloat16)

    def input_term(d):
        at = pl.ds(pl.multiple_of(d * width, 128), width)
        first = lax.dot_general(
            gate_back[...], gate_w[at, :], nt, preferred_element_type=jnp.float32
        )
        return first + lax.dot_general(
            up_back[...], up_w[at, :], nt, preferred_element_type=jnp.float32
        )

    tiles(1, input_term)
    finish(0)
    finish(1)
    for t in range(2):

        def sent_back(n):
            copy = back_copy(t, n + 1, origin_of(n + 1))
            copy.wait_recv()
            copy.wait_send()
            z_copy(t, n + 1, block).wait_send()

        loop(blocks - 1, sent_back)
        loop(chip_count, lambda c: pair_copy(t, c).wait_send())
        loop(chip_count - 1, lambda q: chip_copy(t, q + 1).wait_send())

        def spread_done(n):
            k, q = (n // (chip_count - 1), lax.rem(n, chip_count - 1) + 1)
            spread_copy(t, k, origin_of(k), q, place).wait_send()

        loop(blocks * (chip_count - 1), spread_done)

        def partner_done(n):
            k, q = (n // chip_count, lax.rem(n, chip_count))
            partner_copy(t, k, origin_of(k), q, place).wait_send()

        loop(blocks * chip_count, partner_done)


def experts(cap, send_rows, send_grads, gate_weight, up_weight, down_weight):
    peers, blocks = (lax.axis_size("dp"), lax.axis_size("expert"))
    chip_count = peers // 2
    total, width = send_rows.shape
    features, units = gate_weight.shape[1:]
    half, full = (jnp.bfloat16, jnp.float32)
    vmem = pl.BlockSpec(memory_space=pltpu.VMEM)
    hbm = pl.BlockSpec(memory_space=pl.ANY)
    dma = pltpu.SemaphoreType.DMA
    shapes = [(total, width)] * 2 + [(total, features)] * 2 + [(total, units)] * 3
    return pl.pallas_call(
        functools.partial(expert_kernel, cap),
        out_shape=[jax.ShapeDtypeStruct(shape, half) for shape in shapes],
        in_specs=[vmem, vmem, hbm, hbm, hbm],
        out_specs=[vmem] * 7,
        scratch_shapes=[
            pltpu.VMEM((features, units), half),
            pltpu.VMEM((features, units), half),
            pltpu.VMEM((units, features), half),
            pltpu.VMEM((total, units), full),
            pltpu.VMEM((total, units), full),
            pltpu.VMEM((2, chip_count, total, width), half),
            pltpu.VMEM((2, chip_count, total, width), half),
            pltpu.VMEM((2, chip_count, total, width), half),
            pltpu.VMEM((2, chip_count, total, width), half),
            pltpu.VMEM((2, total, width), half),
            dma((2, blocks)),
            dma((2, blocks)),
            dma((2, blocks * chip_count)),
            dma((2, blocks * chip_count)),
            dma((2, blocks * chip_count)),
            dma((2, blocks * chip_count)),
            dma((2, chip_count)),
            dma((2, chip_count)),
            dma((2, chip_count)),
            dma((2, chip_count)),
            dma((2, blocks)),
            dma((2, blocks)),
            dma((2,)),
            dma((3,)),
        ],
        compiler_params=pltpu.CompilerParams(collective_id=7, has_side_effects=True),
        name="experts",
    )(send_rows, send_grads, gate_weight, up_weight, down_weight)


def body(
    tokens,
    routes,
    dt_raw,
    b_proj,
    c_proj,
    decay_rate,
    skip_gain,
    router_weight,
    gate_weight,
    up_weight,
    down_weight,
    out_grad,
):
    tok_count, width = tokens.shape
    expert_count = lax.axis_size("expert")
    features = width * lax.axis_size("dp")
    head_count = decay_rate.shape[0]
    capacity = 5 * tok_count // (2 * expert_count)
    padded = -(-capacity // 16) * 16
    inputs = tokens.astype(jnp.float32)
    (square_one,) = swap("sum_one", 1, (jnp.sum(inputs * inputs, axis=1)[None], "dp", True))
    scale_one = lax.rsqrt(square_one[0][:, None] / features + EPSILON)
    normed = inputs * scale_one
    decay_total, local_state = end_parts(normed, b_proj, dt_raw, decay_rate)
    state_width = local_state.shape[1]
    packed = jnp.concatenate(
        [local_state, jnp.broadcast_to(decay_total[:, None], (head_count, 128))], axis=1
    )
    (ends,) = swap("state_one", 2, (packed, "expert", False))
    decays = ends[:, :, state_width]
    state_in = carry_in(decays, ends[:, :, :state_width], False)

    def mixer(normed_in, rate_in, skip_in, state_start):
        return ssd_piece(normed_in, b_proj, c_proj, dt_raw, rate_in, skip_in, state_start)

    (mixed, state_end), mixer_pull = jax.vjp(mixer, normed, decay_rate, skip_gain, state_in)
    resid = (inputs + mixed).astype(jnp.bfloat16)
    resid_f = resid.astype(jnp.float32)
    raw_part = lax.dot_general(
        router_weight, resid_f, (((0,), (1,)), ((), ())), precision=HIGHEST
    )
    stats = jnp.concatenate([jnp.sum(resid_f * resid_f, axis=1)[None], raw_part], axis=0)
    (stats,) = swap("sum_two", 3, (stats, "dp", True))
    scale_row = lax.rsqrt(stats[0] / features + EPSILON)
    scale_two = scale_row[:, None]
    moe_in = (resid_f * scale_two).astype(jnp.bfloat16)
    expert_ids = jnp.arange(expert_count, dtype=jnp.int32)
    first_hot = (routes[:, 0:1] == expert_ids[None, :]).astype(jnp.float32)
    second_hot = (routes[:, 1:2] == expert_ids[None, :]).astype(jnp.float32)
    hot_gap = first_hot - second_hot
    raw_gap = jnp.sum(stats[1:].T * hot_gap, axis=1)
    logit_gap = raw_gap * scale_row
    first_weight = jax.nn.sigmoid(logit_gap)
    second_weight = jax.nn.sigmoid(-logit_gap)
    positions = jnp.arange(tok_count, dtype=jnp.int32)
    lower = (positions[:, None] > positions[None, :]).astype(jnp.bfloat16)
    both_hot = (first_hot + second_hot).astype(jnp.bfloat16)
    earlier = jnp.dot(lower, both_hot, preferred_element_type=jnp.float32)

    def slot_of(hot, ids):
        index = jnp.sum(earlier * hot, axis=1)
        target = ids.astype(jnp.float32) * padded + index
        return jnp.where(index < capacity, target, -1.0)

    slot_ids = jnp.arange(expert_count * padded, dtype=jnp.int32).astype(jnp.float32)[:, None]
    first_table = slot_ids == slot_of(first_hot, routes[:, 0])[None, :]
    second_table = slot_ids == slot_of(second_hot, routes[:, 1])[None, :]
    either = (first_table | second_table).astype(jnp.bfloat16)
    slot_weight = jnp.sum(
        jnp.where(first_table, first_weight[None, :], 0.0)
        + jnp.where(second_table, second_weight[None, :], 0.0),
        axis=1,
        keepdims=True,
    )
    send_rows = jnp.dot(either, moe_in, preferred_element_type=jnp.float32).astype(jnp.bfloat16)
    send_grads = jnp.dot(either, out_grad, preferred_element_type=jnp.float32) * slot_weight
    back_f, back_b, unit_rows, grad_rows, hidden, gate_back, up_back = experts(
        padded, send_rows, send_grads.astype(jnp.bfloat16), gate_weight, up_weight, down_weight
    )
    tn = (((0,), (0,)), ((), ()))
    down_part = lax.dot_general(hidden, grad_rows, tn, preferred_element_type=jnp.float32)
    gate_part = lax.dot_general(unit_rows, gate_back, tn, preferred_element_type=jnp.float32)
    up_part = lax.dot_general(unit_rows, up_back, tn, preferred_element_type=jnp.float32)
    pair_table = jnp.concatenate([first_table, second_table], axis=1).astype(jnp.bfloat16)
    per_slot = lax.dot_general(pair_table, back_f, tn, preferred_element_type=jnp.float32)
    first_out, second_out = (per_slot[:tok_count], per_slot[tok_count:])
    moe_sum = first_weight[:, None] * first_out + second_weight[:, None] * second_out
    block_out = (resid_f + moe_sum).astype(jnp.bfloat16)
    moe_grad = lax.dot_general(either, back_b, tn, preferred_element_type=jnp.float32)
    upstream = out_grad.astype(jnp.float32)
    inner_parts = jnp.stack(
        [
            jnp.sum(upstream * first_out, axis=1),
            jnp.sum(upstream * second_out, axis=1),
            jnp.sum(resid_f * moe_grad, axis=1),
        ]
    )
    (inner_all,) = swap("sum_three", 4, (inner_parts, "dp", True))
    gap_grad = first_weight * second_weight * (inner_all[0] - inner_all[1])
    inner = inner_all[2] + gap_grad * raw_gap
    logit_grad = gap_grad[:, None] * hot_gap
    moe_in_grad = moe_grad + jnp.dot(logit_grad, router_weight.T, precision=HIGHEST)
    router_part = lax.dot_general(logit_grad, moe_in.astype(jnp.float32), tn, precision=HIGHEST)
    resid_grad = (
        upstream
        + scale_two * moe_in_grad
        - resid_f * (scale_two * scale_two * scale_two) * (inner[:, None] / features)
    )
    running = jnp.cumsum(-jax.nn.softplus(dt_raw) * decay_rate[None, :], axis=0)
    grad_heads = resid_grad.reshape(tok_count, head_count, -1)
    state_grad = jnp.einsum(
        "th,thp,tn->hpn", jnp.exp(running), grad_heads, c_proj, precision=HIGHEST
    ).reshape(head_count, -1)
    grad_ends, router_total = swap(
        "state_two", 5, (state_grad, "expert", False), (router_part, "expert", True)
    )
    later_grad = carry_in(decays, grad_ends, True)
    normed_grad, rate_part, skip_part, _ = mixer_pull((resid_grad, later_grad))
    inner_one = jnp.sum(normed_grad * inputs, axis=1)[None]
    small = jnp.pad(jnp.stack([rate_part, skip_part]), ((0, 0), (0, 128 - head_count)))
    inner_one, small = swap("sum_four", 6, (inner_one, "dp", True), (small, "expert", True))
    token_grad = (
        resid_grad
        + scale_one * normed_grad
        - inputs * (scale_one * scale_one * scale_one) * (inner_one[0][:, None] / features)
    )
    return (
        block_out,
        token_grad.astype(jnp.bfloat16),
        gate_part.astype(jnp.bfloat16)[None],
        up_part.astype(jnp.bfloat16)[None],
        down_part.astype(jnp.bfloat16)[None],
        router_total.T,
        small[0, :head_count],
        small[1, :head_count],
    )


def solution(mesh):
    return jax.shard_map(
        body,
        mesh=mesh,
        in_specs=(
            P("expert", "dp"),
            P("expert", None),
            P("expert", "dp"),
            P("expert", None),
            P("expert", None),
            P("dp"),
            P("dp"),
            P("dp", None),
            P("expert", None, "dp"),
            P("expert", None, "dp"),
            P("expert", "dp", None),
            P("expert", "dp"),
        ),
        out_specs=(
            P("expert", "dp"),
            P("expert", "dp"),
            P("expert", None, "dp"),
            P("expert", None, "dp"),
            P("expert", "dp", None),
            P("dp", None),
            P("dp"),
            P("dp"),
        ),
        check_vma=False,
    )
```

time: 331 us -> 143 us (0.43)
  blocking collectives: 131 us -> 0 us
  waiting for transfers between devices: 116 us -> 0 us
  Pallas kernels: 0 us -> 90.3 us
  matrix products: 40.8 us -> 25.4 us
  between operations: 14.3 us -> 1.13 us
  starting transfers between devices: 9.5 us -> 0 us
  local copies, waits for them, and re-layouts: 6.81 us -> 11.5 us
    pallas_call x0 -> x7, Pallas kernels: none -> 90.3 us  [the longest x1 49.2 us: experts(): pl.pallas_call(functools.partial(expert_kernel, cap), out_shape=[jax.Shap...]
    psum x6 -> x0, blocking collectives: 73.5 us -> none  [the longest x5 62.6 us: feature_sum(): return lax.psum(values, 'dp')]
    reduce_scatter x2 -> x0, waiting for transfers between devices: 62.5 us -> none  [from_units(): lax.psum_scatter(terms.astype(jnp.bfloat16), 'dp', scatter_dimension=1, t...]
    all_gather x2 -> x0, waiting for transfers between devices: 44.8 us -> none  [to_units(): return lax.all_gather(flat_rows, 'dp', axis=1, tiled=True)]
    all_gather x3 -> x0, blocking collectives: 37.4 us -> none  [carried_in(): everything = jax.tree.map(lambda part: lax.all_gather(part, axis), x)]
    all_to_all x2 -> x0, blocking collectives: 20.1 us -> none  [to_units(): lax.all_to_all(send_rows, 'expert', split_axis=0, concat_axis=0, tiled=True)]
    dot_general x16 -> x11, matrix products: 34 us -> 18.5 us  [the longest x1 4.12 us: body(): lax.dot_general(unit_rows, up_back, tn, preferred_element_type=jnp.float32)]
    all_to_all x2 -> x0, starting transfers between devices: 9.2 us -> none  [from_units(): lax.all_to_all(shaped, 'expert', split_axis=0, concat_axis=0, tiled=True)]
  transfers between devices with their start and end apart: 6 -> 0, of which waited for: 6 -> 0; matrix products, arithmetic and copies ran while one was open for 5% -> 0% of each run, Pallas kernels for 0% -> 0%
where the time goes in v1:
time: 143 us; the launch traced here: 142 us
  Pallas kernels  90.3 us (63%)
  matrix products  25.4 us (18%)
  other arithmetic  13.5 us (9%)
  local copies, waits for them, and re-layouts  11.5 us (8%)
    pallas_call x1, Pallas kernels, experts(): pl.pallas_call(functools.partial(expert_kernel, cap), out_shape=[jax.Shap...  49.2 us
    pallas_call x6, Pallas kernels, swap(): pl.pallas_call(functools.partial(swap_kernel, plan), out_shape=[jax.Shape...  41.1 us
    dot_general x1, matrix products, body(): lax.dot_general(unit_rows, up_back, tn, preferred_element_type=jnp.float32)  4.12 us
    dot_general x1, matrix products, body(): lax.dot_general(unit_rows, gate_back, tn, preferred_element_type=jnp.floa...  4.1 us
    unnamed x33, local copies, waits for them, and re-layouts  4.06 us
    dot_general x1, matrix products, body(): lax.dot_general(hidden, grad_rows, tn, preferred_element_type=jnp.float32)  3.94 us

profile of v1, /device:TPU:0, one launch (start us, length us, event | category | flops | bytes accessed | tf_op | source)
XLA Modules:
  0.0 141.8 jit_solution(1942788650345857372)
XLA Ops:
  0.7 0.8 slice_bitcast_fusion.3
  1.5 0.8 negate_multiply_fusion
  2.9 0.8 compare_select_fusion
  3.6 1.0 copy.97
  4.6 0.6 fusion.23
  5.2 7.4 %sum_one.1 = f32[1,128]{1,0:T(1,128)} custom-call(f32[1,128]{1,0:T(1,128)} %bitcast.225), custom_call_target="tpu_custom_call" | custom-call | tf_op jit(solution)/shard_map/sum_one/pallas_call | solution.py:87
  12.6 0.7 rsqrt_bitcast_fusion
  13.3 0.7 multiply_multiply_fusion.4
  14.0 1.0 fusion.111
  15.0 1.0 copy.106
  16.1 0.9 fusion.64
  17.1 0.6 pad_maximum_fusion.refs_0_
  17.8 7.6 %state_one.1 = f32[4,4,1152]{2,1,0:T(4,128)} custom-call(f32[4,1152]{1,0:T(4,128)} %pad_maximum_fusion.refs_0_), custom_call_target="tpu_custom_call" | custom-call | tf_op jit(solution)/shard_map/state_one/pallas_call | solution.py:87
  25.4 0.8 slice_reduce_fusion.3
  26.2 0.8 fusion.109
  27.5 0.9 convolution_bitcast_fusion.4
  28.5 1.3 fusion.9
  30.0 0.6 pad_maximum_fusion.1.refs_0_
  30.7 6.0 %sum_two.1 = f32[5,128]{1,0:T(8,128)} custom-call(f32[5,128]{1,0:T(8,128)} %pad_maximum_fusion.1.refs_0_), custom_call_target="tpu_custom_call" | custom-call | tf_op jit(solution)/shard_map/sum_two/pallas_call | solution.py:87
  36.6 0.7 multiply_multiply_fusion.5
  37.3 0.8 select_reduce_fusion.1
  38.6 0.9 fusion.5.send_grads
  39.5 0.9 convolution_convert_fusion.send_rows
  40.4 49.2 %experts.1 = (bf16[320,256]{1,0:T(8,128)(2,1)}, bf16[320,256]{1,0:T(8,128)(2,1)}, bf16[320,2048]{1,0:T(8,128)(2,1)}, bf16[320,2048]{1,0:T(8,128)(2,1)}, bf16[320...) custom-call(bf16[320,256]{1,0:T(8,128)(2,1)} %convolution_convert_fusion.send_rows, ...), custom_call_target="tpu_custom_call" | custom-call | tf_op jit(solution)/shard_map/experts/pallas_call | solution.py:430
  89.7 1.2 fusion.17
  91.0 1.3 fusion.32
  92.3 0.6 pad_maximum_fusion.2.refs_0_
  92.8 5.9 %sum_three.1 = f32[3,128]{1,0:T(4,128)} custom-call(f32[3,128]{1,0:T(4,128)} %pad_maximum_fusion.2.refs_0_), custom_call_target="tpu_custom_call" | custom-call | tf_op jit(solution)/shard_map/sum_three/pallas_call | solution.py:87
  98.7 0.8 fusion.102
  100.0 0.8 fusion.58.refs_1_
  101.1 0.7 copy.122
  101.9 0.7 fusion.106
  103.0 1.1 reduce_window_sum.34
  104.5 0.7 reshape.294.refs_0_
  105.2 7.4 %state_two.1 = (f32[4,4,1024]{2,1,0:T(4,128)}, f32[4,256]{1,0:T(4,128)}) custom-call(f32[4,1024]{1,0:T(4,128)} %reshape.294.refs_0_, f32[4,256]{1,0:T(4,128)} %fusion.58.refs_1_), custom_call_target="tpu_custom_call" | custom-call | tf_op jit(solution)/shard_map/state_two/pallas_call | solution.py:87
  112.6 1.0 fusion.70
  113.8 0.8 fusion.110
  116.6 0.6 multiply_reduce_fusion
  117.6 1.1 reduce_window_sum.33
  119.0 0.6 select_maximum_fusion.refs_1_
  119.6 6.8 %sum_four.1 = (f32[1,128]{1,0:T(1,128)}, f32[2,128]{1,0:T(2,128)}) custom-call(f32[1,128]{1,0:T(1,128)} %bitcast.224, f32[2,128]{1,0:T(2,128)} %select_maximum_fusion.refs_1_), custom_call_target="tpu_custom_call" | custom-call | tf_op jit(solution)/shard_map/sum_four/pallas_call | solution.py:87
  126.4 0.6 multiply_bitcast_fusion.2
  127.0 0.7 copy.123
  127.8 1.2 slice_bitcast_fusion
  129.0 4.1 %convert_bitcast_fusion.2 = bf16[1,2048,896]{2,1,0:T(8,128)(2,1)} fusion(bf16[320,2048]{1,0:T(8,128)(2,1)S(1)} %copy-done.9, bf16[320,896]{1,0:T(8,128)(2,1)S(1)} %copy-done.12), kind=kOutput, calls=%fused_computation.2 | convolution fusion | flops 1176240128 | bytes 5554176 | tf_op jit(solution)/shard_map/dot_general | solution.py:548
  133.1 4.1 %convert_bitcast_fusion.1 = bf16[1,2048,896]{2,1,0:T(8,128)(2,1)} fusion(bf16[320,2048]{1,0:T(8,128)(2,1)S(1)} %copy-done.9, bf16[320,896]{1,0:T(8,128)(2,1)S(1)} %copy-done.11), kind=kOutput, calls=%fused_computation.1 | convolution fusion | flops 1176240128 | bytes 5554176 | tf_op jit(solution)/shard_map/dot_general | solution.py:549
  137.2 3.9 %convert_bitcast_fusion = bf16[1,896,2048]{2,1,0:T(8,128)(2,1)} fusion(bf16[320,896]{1,0:T(8,128)(2,1)S(1)} %copy-done.10, bf16[320,2048]{1,0:T(8,128)(2,1)S(1)} %copy-done.8), kind=kOutput, calls=%fused_computation | convolution fusion | flops 1176240128 | bytes 5554176 | tf_op jit(solution)/shard_map/dot_general | solution.py:547
  141.2 0.6 copy.151
  (84 shorter events, 6.4 us)
Async XLA Ops:
  0.6 29.3 %copy-start = (f32[256,4]{0,1:T(4,128)S(1)}, f32[256,4]{0,1:T(4,128)}, u32[]{:S(2)}) copy-start(f32[256,4]{0,1:T(4,128)} %param.19) | copy-start | bytes 12292
  0.6 37.9 %copy-start.4 = (bf16[128,256]{1,0:T(8,128)(2,1)S(1)}, bf16[128,256]{1,0:T(8,128)(2,1)}, u32[]{:S(2)}) copy-start(bf16[128,256]{1,0:T(8,128)(2,1)} %param.23) | copy-start | bytes 196612
  0.7 37.5 %copy-start.6 = (s32[128,2]{0,1:T(2,128)S(1)}, s32[128,2]{0,1:T(2,128)}, u32[]{:S(2)}) copy-start(s32[128,2]{0,1:T(2,128)} %param.13) | copy-start | bytes 3076
  40.4 60.3 %copy-start.2 = (f32[128,16]{0,1:T(8,128)S(1)}, f32[128,16]{0,1:T(8,128)}, u32[]{:S(2)}) copy-start(f32[128,16]{0,1:T(8,128)} %param.16) | copy-start | bytes 24580
  89.6 23.0 %copy-start.1 = (f32[4,4,1152]{2,1,0:T(4,128)S(1)}, f32[4,4,1152]{2,1,0:T(4,128)}, u32[]{:S(2)}) copy-start(f32[4,4,1152]{2,1,0:T(4,128)} %state_one.1) | copy-start | bytes 221188
  89.6 25.5 %copy-start.3 = (f32[128,16]{0,1:T(8,128)S(1)}, f32[128,16]{0,1:T(8,128)}, u32[]{:S(2)}) copy-start(f32[128,16]{0,1:T(8,128)} %param.15) | copy-start | bytes 24580
  89.7 26.1 %copy-start.13 = (f32[4]{0:T(128)S(1)}, f32[4]{0:T(128)}, u32[]{:S(2)}) copy-start(f32[4]{0:T(128)} %param.18) | copy-start | bytes 52
  89.7 26.6 %copy-start.5 = (f32[128,4]{0,1:T(4,128)S(1)}, f32[128,4]{0,1:T(4,128)}, u32[]{:S(2)}) copy-start(f32[128,4]{0,1:T(4,128)} %param.14) | copy-start | bytes 6148
  92.2 36.7 %copy-start.9 = (bf16[320,2048]{1,0:T(8,128)(2,1)S(1)}, bf16[320,2048]{1,0:T(8,128)(2,1)}, u32[]{:S(2)}) copy-start(bf16[320,2048]{1,0:T(8,128)(2,1)} %get-tuple-element.23) | copy-start | bytes 3932164
  92.3 36.7 %copy-start.12 = (bf16[320,896]{1,0:T(8,128)(2,1)S(1)}, bf16[320,896]{1,0:T(8,128)(2,1)}, u32[]{:S(2)}) copy-start(bf16[320,896]{1,0:T(8,128)(2,1)} %get-tuple-element.24) | copy-start | bytes 1720324
  129.0 4.1 %copy-start.11 = (bf16[320,896]{1,0:T(8,128)(2,1)S(1)}, bf16[320,896]{1,0:T(8,128)(2,1)}, u32[]{:S(2)}) copy-start(bf16[320,896]{1,0:T(8,128)(2,1)} %get-tuple-element.25) | copy-start | bytes 1720324
  133.1 4.1 %copy-start.8 = (bf16[320,2048]{1,0:T(8,128)(2,1)S(1)}, bf16[320,2048]{1,0:T(8,128)(2,1)}, u32[]{:S(2)}) copy-start(bf16[320,2048]{1,0:T(8,128)(2,1)} %get-tuple-element.27) | copy-start | bytes 3932164
  133.1 4.1 %copy-start.10 = (bf16[320,896]{1,0:T(8,128)(2,1)S(1)}, bf16[320,896]{1,0:T(8,128)(2,1)}, u32[]{:S(2)}) copy-start(bf16[320,896]{1,0:T(8,128)(2,1)} %get-tuple-element.26) | copy-start | bytes 1720324
  137.2 3.9 %copy-start.7 = (f32[4,256]{1,0:T(4,128)S(1)}, f32[4,256]{1,0:T(4,128)}, u32[]{:S(2)}) copy-start(f32[4,256]{1,0:T(4,128)} %get-tuple-element.28) | copy-start | bytes 12292

commit v2 on v1

--- a/solution.py
+++ b/solution.py
@@ -95,11 +95,17 @@
     )(*arrays)
 
 
+def running_sum(values):
+    positions = jnp.arange(values.shape[0], dtype=jnp.int32)
+    reached = (positions[:, None] >= positions[None, :]).astype(jnp.float32)
+    return jnp.dot(reached, values, precision=HIGHEST)
+
+
 def end_parts(normed, b_rows, dt_rows, decay_rate):
     steps_total = normed.shape[0]
     head_count = decay_rate.shape[0]
     step_size = jax.nn.softplus(dt_rows)
-    running = jnp.cumsum(-step_size * decay_rate[None, :], axis=0)
+    running = running_sum(-step_size * decay_rate[None, :])
     tail_weight = jnp.exp(running[-1][None, :] - running) * step_size
     head_rows = normed.reshape(steps_total, head_count, -1)
     local_state = jnp.einsum("sh,shp,sn->hpn", tail_weight, head_rows, b_rows, precision=HIGHEST)
@@ -111,7 +117,7 @@
     head_count = decay_rate.shape[0]
     state_width = b_rows.shape[1]
     step_size = jax.nn.softplus(dt_rows)
-    running = jnp.cumsum(-step_size * decay_rate[None, :], axis=0)
+    running = running_sum(-step_size * decay_rate[None, :])
     positions = jnp.arange(steps_total, dtype=jnp.int32)
     causal = (positions[:, None] >= positions[None, :])[:, :, None]
     spread = jnp.where(causal, running[:, None, :] - running[None, :, :], 0.0)
@@ -572,7 +578,7 @@
         + scale_two * moe_in_grad
         - resid_f * (scale_two * scale_two * scale_two) * (inner[:, None] / features)
     )
-    running = jnp.cumsum(-jax.nn.softplus(dt_raw) * decay_rate[None, :], axis=0)
+    running = running_sum(-jax.nn.softplus(dt_raw) * decay_rate[None, :])
     grad_heads = resid_grad.reshape(tok_count, head_count, -1)
     state_grad = jnp.einsum(
         "th,thp,tn->hpn", jnp.exp(running), grad_heads, c_proj, precision=HIGHEST

time: 143 us -> 140 us (0.979)
  other arithmetic: 13.5 us -> 10 us
  matrix products: 25.4 us -> 26.9 us
    another operation x3 -> x0, other arithmetic: 2.4 us -> none  [the longest x2 1.29 us: ssd_piece(): running = jnp.cumsum(-step_size * decay_rate[None, :], axis=0)]
    dot_general x0 -> x3, matrix products: none -> 1.44 us  [running_sum(): return jnp.dot(reached, values, precision=HIGHEST)]
where the time goes in v2:
time: 140 us; the launch traced here: 139 us
  Pallas kernels  90.3 us (64%)
  matrix products  26.9 us (19%)
  local copies, waits for them, and re-layouts  10.6 us (8%)
  other arithmetic  10 us (7%)
    pallas_call x1, Pallas kernels, experts(): pl.pallas_call(functools.partial(expert_kernel, cap), out_shape=[jax.Shap...  49.2 us
    pallas_call x6, Pallas kernels, swap(): pl.pallas_call(functools.partial(swap_kernel, plan), out_shape=[jax.Shape...  41.1 us
    dot_general x1, matrix products, body(): lax.dot_general(unit_rows, up_back, tn, preferred_element_type=jnp.float32)  4.12 us
    dot_general x1, matrix products, body(): lax.dot_general(unit_rows, gate_back, tn, preferred_element_type=jnp.floa...  4.1 us
    unnamed x33, local copies, waits for them, and re-layouts  4.05 us
    dot_general x1, matrix products, body(): lax.dot_general(hidden, grad_rows, tn, preferred_element_type=jnp.float32)  3.95 us

profile of v2, /device:TPU:0, one launch (start us, length us, event | category | flops | bytes accessed | tf_op | source)
XLA Modules:
  0.0 139.0 jit_solution(3272127288897134153)
XLA Ops:
  0.7 0.8 slice_bitcast_fusion.3
  1.5 0.9 fusion.63
  2.6 0.8 compare_select_fusion
  3.4 1.0 copy.52
  4.4 0.6 fusion.25
  5.0 7.4 %sum_one.1 = f32[1,128]{1,0:T(1,128)} custom-call(f32[1,128]{1,0:T(1,128)} %bitcast.225), custom_call_target="tpu_custom_call" | custom-call | tf_op jit(solution)/shard_map/sum_one/pallas_call | solution.py:87
  12.4 0.7 rsqrt_bitcast_fusion
  13.1 0.7 multiply_multiply_fusion.4
  13.8 1.0 fusion.128
  14.8 1.0 copy.55
  15.8 0.9 fusion.67
  16.8 0.6 pad_maximum_fusion.refs_0_
  17.4 7.6 %state_one.1 = f32[4,4,1152]{2,1,0:T(4,128)} custom-call(f32[4,1152]{1,0:T(4,128)} %pad_maximum_fusion.refs_0_), custom_call_target="tpu_custom_call" | custom-call | tf_op jit(solution)/shard_map/state_one/pallas_call | solution.py:87
  25.0 0.8 slice_reduce_fusion.3
  25.9 0.8 fusion.126
  27.2 0.9 convolution_bitcast_fusion.4
  28.2 1.3 fusion.9
  29.7 0.6 pad_maximum_fusion.1.refs_0_
  30.3 6.0 %sum_two.1 = f32[5,128]{1,0:T(8,128)} custom-call(f32[5,128]{1,0:T(8,128)} %pad_maximum_fusion.1.refs_0_), custom_call_target="tpu_custom_call" | custom-call | tf_op jit(solution)/shard_map/sum_two/pallas_call | solution.py:87
  36.3 0.7 multiply_multiply_fusion.5
  37.0 0.8 select_reduce_fusion.1
  38.3 0.9 fusion.5.send_grads
  39.2 0.9 convolution_convert_fusion.send_rows
  40.1 49.2 %experts.1 = (bf16[320,256]{1,0:T(8,128)(2,1)}, bf16[320,256]{1,0:T(8,128)(2,1)}, bf16[320,2048]{1,0:T(8,128)(2,1)}, bf16[320,2048]{1,0:T(8,128)(2,1)}, bf16[320...) custom-call(bf16[320,256]{1,0:T(8,128)(2,1)} %convolution_convert_fusion.send_rows, ...), custom_call_target="tpu_custom_call" | custom-call | tf_op jit(solution)/shard_map/experts/pallas_call | solution.py:436
  89.4 1.3 fusion.19
  90.8 1.3 fusion.34
  92.1 0.6 pad_maximum_fusion.2.refs_0_
  92.6 5.9 %sum_three.1 = f32[3,128]{1,0:T(4,128)} custom-call(f32[3,128]{1,0:T(4,128)} %pad_maximum_fusion.2.refs_0_), custom_call_target="tpu_custom_call" | custom-call | tf_op jit(solution)/shard_map/sum_three/pallas_call | solution.py:87
  98.5 0.8 fusion.117
  99.4 0.4 fusion.12
  99.8 0.8 fusion.60.refs_1_
  100.9 0.7 copy.65
  101.7 0.7 fusion.124
  102.9 0.7 reshape.294.refs_0_
  103.6 7.4 %state_two.1 = (f32[4,4,1024]{2,1,0:T(4,128)}, f32[4,256]{1,0:T(4,128)}) custom-call(f32[4,1024]{1,0:T(4,128)} %reshape.294.refs_0_, f32[4,256]{1,0:T(4,128)} %fusion.60.refs_1_), custom_call_target="tpu_custom_call" | custom-call | tf_op jit(solution)/shard_map/state_two/pallas_call | solution.py:87
  111.0 1.0 fusion.73
  112.2 0.8 fusion.127
  114.2 0.5 fusion.7
  115.3 0.6 multiply_reduce_fusion
  116.2 0.6 select_maximum_fusion.refs_1_
  116.7 6.8 %sum_four.1 = (f32[1,128]{1,0:T(1,128)}, f32[2,128]{1,0:T(2,128)}) custom-call(f32[1,128]{1,0:T(1,128)} %bitcast.224, f32[2,128]{1,0:T(2,128)} %select_maximum_fusion.refs_1_), custom_call_target="tpu_custom_call" | custom-call | tf_op jit(solution)/shard_map/sum_four/pallas_call | solution.py:87
  123.6 0.6 multiply_bitcast_fusion.2
  124.2 0.7 copy.66
  124.9 1.2 slice_bitcast_fusion
  126.2 4.1 %convert_bitcast_fusion.2 = bf16[1,2048,896]{2,1,0:T(8,128)(2,1)} fusion(bf16[320,2048]{1,0:T(8,128)(2,1)S(1)} %copy-done.9, bf16[320,896]{1,0:T(8,128)(2,1)S(1)} %copy-done.12), kind=kOutput, calls=%fused_computation.2 | convolution fusion | flops 1176240128 | bytes 5554176 | tf_op jit(solution)/shard_map/dot_general | solution.py:554
  130.3 4.1 %convert_bitcast_fusion.1 = bf16[1,2048,896]{2,1,0:T(8,128)(2,1)} fusion(bf16[320,2048]{1,0:T(8,128)(2,1)S(1)} %copy-done.9, bf16[320,896]{1,0:T(8,128)(2,1)S(1)} %copy-done.11), kind=kOutput, calls=%fused_computation.1 | convolution fusion | flops 1176240128 | bytes 5554176 | tf_op jit(solution)/shard_map/dot_general | solution.py:555
  134.4 3.9 %convert_bitcast_fusion = bf16[1,896,2048]{2,1,0:T(8,128)(2,1)} fusion(bf16[320,896]{1,0:T(8,128)(2,1)S(1)} %copy-done.10, bf16[320,2048]{1,0:T(8,128)(2,1)S(1)} %copy-done.8), kind=kOutput, calls=%fused_computation | convolution fusion | flops 1176240128 | bytes 5554176 | tf_op jit(solution)/shard_map/dot_general | solution.py:553
  138.4 0.6 copy.93
  (68 shorter events, 4.8 us)
Async XLA Ops:
  0.6 29.0 %copy-start = (f32[256,4]{0,1:T(4,128)S(1)}, f32[256,4]{0,1:T(4,128)}, u32[]{:S(2)}) copy-start(f32[256,4]{0,1:T(4,128)} %param.19) | copy-start | bytes 12292
  0.6 37.6 %copy-start.4 = (bf16[128,256]{1,0:T(8,128)(2,1)S(1)}, bf16[128,256]{1,0:T(8,128)(2,1)}, u32[]{:S(2)}) copy-start(bf16[128,256]{1,0:T(8,128)(2,1)} %param.23) | copy-start | bytes 196612
  0.7 37.2 %copy-start.6 = (s32[128,2]{0,1:T(2,128)S(1)}, s32[128,2]{0,1:T(2,128)}, u32[]{:S(2)}) copy-start(s32[128,2]{0,1:T(2,128)} %param.13) | copy-start | bytes 3076
  40.1 60.5 %copy-start.2 = (f32[128,16]{0,1:T(8,128)S(1)}, f32[128,16]{0,1:T(8,128)}, u32[]{:S(2)}) copy-start(f32[128,16]{0,1:T(8,128)} %param.16) | copy-start | bytes 24580
  40.1 62.3 %copy-start.5 = (f32[128,4]{0,1:T(4,128)S(1)}, f32[128,4]{0,1:T(4,128)}, u32[]{:S(2)}) copy-start(f32[128,4]{0,1:T(4,128)} %param.14) | copy-start | bytes 6148
  89.3 21.7 %copy-start.1 = (f32[4,4,1152]{2,1,0:T(4,128)S(1)}, f32[4,4,1152]{2,1,0:T(4,128)}, u32[]{:S(2)}) copy-start(f32[4,4,1152]{2,1,0:T(4,128)} %state_one.1) | copy-start | bytes 221188
  89.3 24.2 %copy-start.3 = (f32[128,16]{0,1:T(8,128)S(1)}, f32[128,16]{0,1:T(8,128)}, u32[]{:S(2)}) copy-start(f32[128,16]{0,1:T(8,128)} %param.15) | copy-start | bytes 24580
  89.4 24.8 %copy-start.13 = (f32[4]{0:T(128)S(1)}, f32[4]{0:T(128)}, u32[]{:S(2)}) copy-start(f32[4]{0:T(128)} %param.18) | copy-start | bytes 52
  89.4 36.8 %copy-start.9 = (bf16[320,2048]{1,0:T(8,128)(2,1)S(1)}, bf16[320,2048]{1,0:T(8,128)(2,1)}, u32[]{:S(2)}) copy-start(bf16[320,2048]{1,0:T(8,128)(2,1)} %get-tuple-element.23) | copy-start | bytes 3932164
  89.4 36.8 %copy-start.12 = (bf16[320,896]{1,0:T(8,128)(2,1)S(1)}, bf16[320,896]{1,0:T(8,128)(2,1)}, u32[]{:S(2)}) copy-start(bf16[320,896]{1,0:T(8,128)(2,1)} %get-tuple-element.24) | copy-start | bytes 1720324
  126.2 4.1 %copy-start.11 = (bf16[320,896]{1,0:T(8,128)(2,1)S(1)}, bf16[320,896]{1,0:T(8,128)(2,1)}, u32[]{:S(2)}) copy-start(bf16[320,896]{1,0:T(8,128)(2,1)} %get-tuple-element.25) | copy-start | bytes 1720324
  130.3 4.1 %copy-start.8 = (bf16[320,2048]{1,0:T(8,128)(2,1)S(1)}, bf16[320,2048]{1,0:T(8,128)(2,1)}, u32[]{:S(2)}) copy-start(bf16[320,2048]{1,0:T(8,128)(2,1)} %get-tuple-element.27) | copy-start | bytes 3932164
  130.3 4.1 %copy-start.10 = (bf16[320,896]{1,0:T(8,128)(2,1)S(1)}, bf16[320,896]{1,0:T(8,128)(2,1)}, u32[]{:S(2)}) copy-start(bf16[320,896]{1,0:T(8,128)(2,1)} %get-tuple-element.26) | copy-start | bytes 1720324
  134.4 4.0 %copy-start.7 = (f32[4,256]{1,0:T(4,128)S(1)}, f32[4,256]{1,0:T(4,128)}, u32[]{:S(2)}) copy-start(f32[4,256]{1,0:T(4,128)} %get-tuple-element.28) | copy-start | bytes 12292
